TPU v7x, 32 devices: a whole 2x2x4 slice. The times are simulated.
32 devices in a mesh: dp: 4 (over z), expert: 4 (over y, x), tensor: 2 (over core).
Axes of the slice: x: 2, y: 2, z: 4, core: 2. Of those that a mesh axis runs over, the one named last changes fastest.
Arguments:
- tokens: bfloat16 [512, 6144], P('dp', 'tensor'), may hold values from -6 to 6
- out_grad: bfloat16 [512, 6144], P('dp', 'tensor'), may hold values from -6 to 6
- router_weight: bfloat16 [6144, 4], P('tensor'), may hold values from -0.078125 to 0.078125
- gate_weight: bfloat16 [4, 6144, 8192], P('expert', 'tensor', 'dp'), may hold values from -0.078125 to 0.078125
- up_weight: bfloat16 [4, 6144, 8192], P('expert', 'tensor', 'dp'), may hold values from -0.078125 to 0.078125
- down_weight: bfloat16 [4, 8192, 6144], P('expert', 'dp', 'tensor'), may hold values from -0.0625 to 0.0625
- expert_index: int32 [512, 2], P('dp'), may hold values from 0 to 3, as said below
- slot_index: int32 [512, 2], P('dp'), may hold values from 0 to 95, as said below
Outputs:
- tokens_grad: bfloat16 [512, 6144], P(('dp', 'expert'), 'tensor')
- router_grad: float32 [6144, 4], P('tensor')
- gate_grad: bfloat16 [4, 6144, 8192], P('expert', 'tensor', 'dp')
- up_grad: bfloat16 [4, 6144, 8192], P('expert', 'tensor', 'dp')
- down_grad: bfloat16 [4, 8192, 6144], P('expert', 'dp', 'tensor')
Inputs may be any that keep to these rules, and one draw needn't show every extreme that they name: `expert_index`: each row names two different experts; in each aligned block of 128 rows no expert is named more than 96 times, and one expert is named exactly 96 times in every block. `slot_index`: entry k of a row is a slot of the expert in entry k of the same row of expert_index; within one aligned block of 128 rows the choices of one expert have distinct slots.
All inputs are finite; a program needn't handle non-finite values.
Results may differ from a plain program's by a relative error of at most 0.025.
Values may be sent and summed in bfloat16 or wider, within the bound.
A program may use at most 128 MiB of HBM per device.

v0:
```python
import jax
import jax.numpy as jnp
from jax import lax
from jax.sharding import PartitionSpec as P

CAP = 96
highest = lax.Precision.HIGHEST


def contract_rows(left_side, right_side):
    return lax.dot_general(
        left_side, right_side, (((0,), (0,)), ((), ())), preferred_element_type=jnp.float32
    )


def contract_cols(left_side, right_side):
    return lax.dot_general(
        left_side, right_side, (((1,), (1,)), ((), ())), preferred_element_type=jnp.float32
    )


def split_parts(values):
    high_part = values.astype(jnp.bfloat16)
    low_part = (values - high_part.astype(jnp.float32)).astype(jnp.bfloat16)
    return (high_part, low_part)


def table_apply(form, table_low, values):
    high_part, low_part = split_parts(values)
    return jnp.einsum(form, table_low, high_part, preferred_element_type=jnp.float32) + jnp.einsum(
        form, table_low, low_part, preferred_element_type=jnp.float32
    )


def slot_table(experts_here, slots_here, expert_id, capacity):
    positions = lax.broadcasted_iota(jnp.int32, (capacity, experts_here.shape[0]), 0)
    first_table = (experts_here[:, 0] == expert_id)[None, :] & (
        slots_here[:, 0][None, :] == positions
    )
    second_table = (experts_here[:, 1] == expert_id)[None, :] & (
        slots_here[:, 1][None, :] == positions
    )
    return (first_table.astype(jnp.float32), second_table.astype(jnp.float32))


def hidden_terms(gate_sum, up_sum, grad_act, slot_prob):
    gate_sigmoid = jax.nn.sigmoid(gate_sum)
    hidden = (gate_sum * gate_sigmoid * up_sum).astype(jnp.bfloat16)
    prob_grad = jnp.sum(hidden.astype(jnp.float32) * grad_act, axis=1)
    act_grad = slot_prob.astype(jnp.float32)[:, None] * grad_act
    grad_gate = (act_grad * up_sum * gate_sigmoid * (1.0 + gate_sum * (1.0 - gate_sigmoid))).astype(
        jnp.bfloat16
    )
    grad_up = (act_grad * gate_sum * gate_sigmoid).astype(jnp.bfloat16)
    return (hidden, grad_gate, grad_up, prob_grad)


def shards(
    tokens, out_grad, router_weight, gate_weight, up_weight, down_weight, expert_index, slot_index
):
    capacity = CAP
    expert_count = router_weight.shape[1]
    expert_id = lax.axis_index("expert")
    logits = lax.psum(jnp.dot(tokens, router_weight, preferred_element_type=jnp.float32), "tensor")
    chosen = jnp.take_along_axis(logits, expert_index, axis=1)
    pick_prob = jnp.stack(
        [jax.nn.sigmoid(chosen[:, 0] - chosen[:, 1]), jax.nn.sigmoid(chosen[:, 1] - chosen[:, 0])],
        axis=1,
    )
    prob_wide = pick_prob.astype(jnp.bfloat16).astype(jnp.float32)
    first_table, second_table = slot_table(expert_index, slot_index, expert_id, capacity)
    select = first_table + second_table
    select_low = select.astype(jnp.bfloat16)
    local_tokens = jnp.dot(select_low, tokens, preferred_element_type=jnp.float32).astype(
        jnp.bfloat16
    )
    local_grads = jnp.dot(select_low, out_grad, preferred_element_type=jnp.float32).astype(
        jnp.bfloat16
    )
    local_prob = (
        jnp.dot(first_table, prob_wide[:, 0], precision=highest)
        + jnp.dot(second_table, prob_wide[:, 1], precision=highest)
    ).astype(jnp.bfloat16)
    slot_tokens, slot_grads, slot_prob = (
        lax.all_gather(local_tokens, "dp", axis=0, tiled=True),
        lax.all_gather(local_grads, "dp", axis=0, tiled=True),
        lax.all_gather(local_prob, "dp", axis=0, tiled=True),
    )
    gate_block = gate_weight[0]
    up_block = up_weight[0]
    down_block = down_weight[0]
    gate_part = jnp.dot(slot_tokens, gate_block, preferred_element_type=jnp.float32)
    up_part = jnp.dot(slot_tokens, up_block, preferred_element_type=jnp.float32)
    grad_part = contract_cols(slot_grads, down_block)
    gate_sum, up_sum, grad_sum = (
        lax.psum(gate_part.astype(jnp.bfloat16), "tensor").astype(jnp.float32),
        lax.psum(up_part.astype(jnp.bfloat16), "tensor").astype(jnp.float32),
        lax.psum(grad_part.astype(jnp.bfloat16), "tensor").astype(jnp.float32),
    )
    hidden, grad_gate, grad_up, prob_grad = hidden_terms(gate_sum, up_sum, grad_sum, slot_prob)
    scaled_grads = (slot_prob.astype(jnp.float32)[:, None] * slot_grads.astype(jnp.float32)).astype(
        jnp.bfloat16
    )
    down_grad = contract_rows(hidden, scaled_grads).astype(jnp.bfloat16)
    gate_grad = contract_rows(slot_tokens, grad_gate).astype(jnp.bfloat16)
    up_grad = contract_rows(slot_tokens, grad_up).astype(jnp.bfloat16)
    slot_dx = contract_cols(grad_gate, gate_block) + contract_cols(grad_up, up_block)
    own_expert = (lax.broadcasted_iota(jnp.int32, (1, expert_count), 1) == expert_id).astype(
        jnp.float32
    )
    row_dx, row_prob = (
        lax.psum_scatter(
            slot_dx.astype(jnp.bfloat16), "dp", scatter_dimension=0, tiled=True
        ).astype(jnp.float32),
        lax.psum_scatter(
            prob_grad.astype(jnp.bfloat16), "dp", scatter_dimension=0, tiled=True
        ).astype(jnp.float32),
    )
    token_dx = table_apply("cn,cd->nd", select_low, row_dx)
    token_prob = table_apply("cn,c->n", select_low, row_prob)
    token_term, prob_rows = (
        lax.psum_scatter(
            token_dx.astype(jnp.bfloat16), "expert", scatter_dimension=0, tiled=True
        ).astype(jnp.float32),
        lax.psum_scatter(
            (token_prob[:, None] * own_expert).astype(jnp.bfloat16),
            "expert",
            scatter_dimension=0,
            tiled=True,
        ).astype(jnp.float32),
    )
    quarter = token_term.shape[0]
    offset = expert_id * quarter
    part_prob = lax.dynamic_slice_in_dim(pick_prob, offset, quarter, 0)
    part_experts = lax.dynamic_slice_in_dim(expert_index, offset, quarter, 0)
    part_tokens = lax.dynamic_slice_in_dim(tokens, offset, quarter, 0)
    pick_grad = jnp.take_along_axis(prob_rows, part_experts, axis=1)
    mixed_grad = jnp.sum(part_prob * pick_grad, axis=1, keepdims=True)
    weights = part_prob * (pick_grad - mixed_grad)
    onehot = (
        part_experts[:, :, None] == lax.broadcasted_iota(jnp.int32, (1, 1, expert_count), 2)
    ).astype(jnp.float32)
    logit_grad = jnp.sum(onehot * weights[:, :, None], axis=1)
    router_rows = router_weight.astype(jnp.float32)
    tokens_grad = (token_term + jnp.dot(logit_grad, router_rows.T, precision=highest)).astype(
        jnp.bfloat16
    )
    router_part = jnp.dot(part_tokens.astype(jnp.float32).T, logit_grad, precision=highest)
    router_grad = lax.psum(router_part, ("dp", "expert"))
    return (tokens_grad, router_grad, gate_grad[None], up_grad[None], down_grad[None])


def solution(mesh):
    in_specs = (
        P("dp", "tensor"),
        P("dp", "tensor"),
        P("tensor", None),
        P("expert", "tensor", "dp"),
        P("expert", "tensor", "dp"),
        P("expert", "dp", "tensor"),
        P("dp", None),
        P("dp", None),
    )
    out_specs = (
        P(("dp", "expert"), "tensor"),
        P("tensor", None),
        P("expert", "tensor", "dp"),
        P("expert", "tensor", "dp"),
        P("expert", "dp", "tensor"),
    )
    return jax.shard_map(shards, mesh=mesh, in_specs=in_specs, out_specs=out_specs, check_vma=False)
```

profile of v0, /device:TPU:0, one launch (start us, length us, event | category | flops | bytes accessed | tf_op | source)
XLA Modules:
  0.0 356.0 jit_solution(7405413484927864889)
XLA Ops:
  7.2 0.0 copy-start
  7.2 0.0 all-gather.5.cloned.1.call-start
  7.2 0.8 slice_bitcast_fusion.1
  8.0 0.8 compare_bitcast_fusion.1
  8.8 1.1 convolution_convert_fusion
  9.9 0.0 all-gather.5.cloned.1.call-update
  9.9 0.0 all-gather.3.cloned.1.call-start
  10.0 2.3 convolution_convert_fusion.1
  12.2 0.0 all-gather.3.cloned.1.call-update
  12.3 0.0 all-reduce.6.cloned.1.call-start
  12.3 50.6 %all-gather.5.cloned.1.call-done = bf16[384,3072]{1,0:T(8,128)(2,1)} async-done(((bf16[96,3072]{1,0:T(8,128)(2,1)}), bf16[384,3072]{1,0:T(8,128)(2,1)}) %all-gather.5.cloned.1.call-update) | async-done | bytes 2359312 | tf_op jit(solution)/shard_map/all_gather | solution.py:85
  62.9 11.3 %fusion.31 = bf16[384,2048]{1,0:T(8,128)(2,1)} fusion(bf16[384,3072]{1,0:T(8,128)(2,1)} %all-gather.5.cloned.1.call-done, bf16[1,3072,2048]{2,1,0:T(8,128)(2,1)} %param.11), kind=kOutput, calls=%fused_computation.44 | convolution fusion | flops 4832624640 | bytes 16515072 | tf_op jit(solution)/shard_map/dot_general | solution.py:92
  74.1 9.4 %fusion.28 = bf16[384,2048]{1,0:T(8,128)(2,1)} fusion(bf16[384,3072]{1,0:T(8,128)(2,1)S(1)} %copy-done.8, bf16[1,3072,2048]{2,1,0:T(8,128)(2,1)} %param.12), kind=kOutput, calls=%fused_computation.43 | convolution fusion | flops 4832624640 | bytes 16515072 | tf_op jit(solution)/shard_map/dot_general | solution.py:93
  83.5 30.3 %all-gather.3.cloned.1.call-done = bf16[384,3072]{1,0:T(8,128)(2,1)} async-done(((bf16[96,3072]{1,0:T(8,128)(2,1)}), bf16[384,3072]{1,0:T(8,128)(2,1)}) %all-gather.3.cloned.1.call-update) | async-done | bytes 2359312 | tf_op jit(solution)/shard_map/all_gather | solution.py:86
  113.8 9.6 %fusion.25 = bf16[384,2048]{1,0:T(8,128)(2,1)} fusion(bf16[384,3072]{1,0:T(8,128)(2,1)} %all-gather.3.cloned.1.call-done, bf16[1,2048,3072]{2,1,0:T(8,128)(2,1)} %param.13), kind=kOutput, calls=%fused_computation.42 | convolution fusion | flops 4832624640 | bytes 16515072 | tf_op jit(solution)/shard_map/dot_general | solution.py:17
  123.4 0.0 all-reduce.6.cloned.1.call-update
  123.5 0.0 reduce-scatter.6.cloned.1.call-start
  123.5 0.6 copy-done.6
  124.1 0.1 copy.59
  124.2 0.1 reshape.58
  124.4 0.3 fusion.66
  124.7 2.5 psum.35
  127.2 2.4 gather_fusion
  129.5 0.1 reshape.61
  129.7 0.1 copy.60
  129.7 0.6 fusion.65
  131.1 0.1 convolution_bitcast_fusion.3
  131.2 0.1 fusion.37
  131.3 0.2 dynamic-update-slice
  131.5 20.0 %all-reduce.6.cloned.1.call-done = (bf16[384,2048]{1,0:T(8,128)(2,1)}, bf16[384,2048]{1,0:T(8,128)(2,1)}, bf16[384,2048]{1,0:T(8,128)(2,1)}) async-done(((bf16[384,2048]{1,0:T(8,128)(2,1)}, bf16[384,2048]{1,0:T(8,128)(2,1)}, bf16[384,2048]{1,0:T(8,128)(2,1)}), (bf16[384,2048]{1,0:T(8,128)(2,1)}, bf16[384,2048]{1,0:T(8,128)(2,1)}, bf16[384,2048]{1,0:T(8,128)(2,1)})) %all-reduce.6.cloned.1.call-update) | async-done | bytes 4718608 | tf_op jit(solution)/shard_map/psum | solution.py:98
  151.5 3.7 %fusion.14 = bf16[384]{0:T(512)(128)(2,1)S(1)} fusion(bf16[384,2048]{1,0:T(8,128)(2,1)} %get-tuple-element.7, bf16[384,2048]{1,0:T(8,128)(2,1)} %get-tuple-element.8, bf16[384,2048]{1,0:T(8,128)(2,1)} %get-tuple-element.9), kind=kLoop, calls=%fused_computation.31 | loop fusion | flops 9436800 | bytes 4719360 | tf_op jit(solution)/shard_map/reduce_sum | solution.py:49
  155.2 12.1 %all-reduce.2 = (bf16[384]{0:T(512)(128)(2,1)S(1)}, bf16[384]{0:T(512)(128)(2,1)S(1)}) all-reduce(bf16[384]{0:T(512)(128)(2,1)S(1)} %fusion.14, bf16[384]{0:T(512)(128)(2,1)S(1)} %dynamic-update-slice), channel_id=4, replica_groups=mesh['dp'=4,'expert'=4,'tensor'=2] {'dp'}, use_global_device_ids=true, to_apply=%region_7.8.clone | all-reduce | flops 768 | bytes 3072
  167.4 12.2 %fusion = f32[384,3072]{1,0:T(8,128)} fusion(bf16[1,3072,2048]{2,1,0:T(8,128)(2,1)} %param.11, bf16[384,2048]{1,0:T(8,128)(2,1)S(1)} %copy-done.1, bf16[384,2048]{1,0:T(8,128)(2,1)} %get-tuple-element.7, bf16[384,2048]{1,0:T(8,128)(2,1)} %get-tuple-element.9, f32[384]{0:T(512)S(1)} %convert_element_type.124), kind=kOutput, calls=%fused_computation.2 | convolution fusion | flops 4842848256 | bytes 22021632 | tf_op jit(solution)/shard_map/dot_general | solution.py:17
  179.6 16.1 %add_convert_fusion = bf16[384,3072]{1,0:T(8,128)(2,1)} fusion(f32[384,3072]{1,0:T(8,128)} %fusion, bf16[1,3072,2048]{2,1,0:T(8,128)(2,1)} %param.12, bf16[384,2048]{1,0:T(8,128)(2,1)S(1)} %copy-done.2, bf16[384,2048]{1,0:T(8,128)(2,1)} %get-tuple-element.7, f32[384]{0:T(512)S(1)} %convert_element_type.124), kind=kOutput, calls=%fused_computation.20 | convolution fusion | flops 4841275392 | bytes 22808064 | tf_op jit(solution)/shard_map/dot_general | solution.py:17
  195.7 0.0 reduce-scatter.6.cloned.1.call-update
  195.7 0.0 reduce-scatter.10.cloned.1.call-start
  195.8 0.1 bitcast_or_fusion
  195.9 0.1 copy.61
  196.0 0.1 reshape.64
  196.8 0.2 convolution_bitcast_fusion.1
  197.0 0.2 fusion.35
  197.1 0.1 multiply_convert_fusion.2
  197.2 0.7 copy.63
  198.0 0.0 reduce-scatter.10.cloned.1.call-update
  198.0 0.3 reduce-scatter.8.cloned.1.call-start
  198.3 13.5 %convert_bitcast_fusion.2 = bf16[1,3072,2048]{2,1,0:T(8,128)(2,1)} fusion(bf16[384,3072]{1,0:T(8,128)(2,1)} %all-gather.5.cloned.1.call-done, bf16[384,2048]{1,0:T(8,128)(2,1)S(1)} %copy-done.1, bf16[384,2048]{1,0:T(8,128)(2,1)} %get-tuple-element.7, bf16[384,2048]{1,0:T(8,128)(2,1)} %get-tuple-element.9, f32[384]{0:T(512)S(1)} %convert_element_type.124), kind=kOutput, calls=%fused_computation.14 | convolution fusion | flops 4849139712 | bytes 19662336 | tf_op jit(solution)/shard_map/dot_general | solution.py:11
  211.8 0.0 copy-done.4
  211.8 0.0 copy-done.9
  211.8 10.3 %convert_bitcast_fusion.1 = bf16[1,3072,2048]{2,1,0:T(8,128)(2,1)} fusion(bf16[384,3072]{1,0:T(8,128)(2,1)S(1)} %copy-done.9, bf16[384,2048]{1,0:T(8,128)(2,1)S(1)} %copy-done.3, bf16[384,2048]{1,0:T(8,128)(2,1)S(1)} %copy-done.4, f32[384]{0:T(512)S(1)} %convert_element_type.124), kind=kOutput, calls=%fused_computation.13 | convolution fusion | flops 4845207552 | bytes 18089472 | tf_op jit(solution)/shard_map/dot_general | solution.py:11
  222.1 19.6 %reduce-scatter.6.cloned.1.call-done = bf16[96,3072]{1,0:T(8,128)(2,1)} async-done(((bf16[384,3072]{1,0:T(8,128)(2,1)}), bf16[96,3072]{1,0:T(8,128)(2,1)}) %reduce-scatter.6.cloned.1.call-update) | async-done | bytes 589840 | tf_op jit(solution)/shard_map/reduce_scatter | solution.py:112
  241.8 1.5 fusion.48
  243.2 2.4 fusion.12
  245.6 0.0 reduce-scatter.8.cloned.1.call-update
  245.6 12.1 %convert_bitcast_fusion = bf16[1,2048,3072]{2,1,0:T(8,128)(2,1)} fusion(bf16[384,3072]{1,0:T(8,128)(2,1)} %all-gather.3.cloned.1.call-done, f32[384]{0:T(512)S(1)} %convert_element_type.124, bf16[384,2048]{1,0:T(8,128)(2,1)S(1)} %copy-done.1, bf16[384,2048]{1,0:T(8,128)(2,1)} %get-tuple-element.9), kind=kOutput, calls=%fused_computation.12 | convolution fusion | flops 4847960064 | bytes 18089472 | tf_op jit(solution)/shard_map/dot_general | solution.py:11
  257.7 10.6 %reduce-scatter.10.cloned.1.call-done = bf16[32,4]{1,0:T(8,128)(2,1)} async-done(((bf16[128,4]{1,0:T(8,128)(2,1)}), bf16[32,4]{1,0:T(8,128)(2,1)}) %reduce-scatter.10.cloned.1.call-update) | async-done | bytes 272
  268.4 0.8 copy.64
  269.2 0.9 gather_fusion.1
  270.0 0.1 reshape.67
  270.1 0.1 copy.62
  270.2 0.1 multiply_reduce_fusion
  270.3 0.1 subtract_multiply_fusion
  270.4 0.2 fusion.38
  270.6 76.5 %psum.39 = f32[3072,4]{0,1:T(4,128)} all-reduce(f32[3072,4]{0,1:T(4,128)S(1)} %fusion.38), channel_id=1, replica_groups=mesh['dp'=4,'expert'=4,'tensor'=2] {'dp','expert'}, use_global_device_ids=true, to_apply=%region_11.12 | all-reduce | flops 12288 | bytes 98304 | tf_op jit(solution)/shard_map/psum | solution.py:149
  347.1 2.0 fusion.13
  (27 shorter events, 0.1 us)
Async XLA Ops:
  7.2 1.6 copy-start
  7.2 55.7 %all-gather.5.cloned.1.call-start = ((), (), s32[]{:S(2)}) async-start(), calls=%async_computation.4 | async-start | bytes 2949120 | tf_op jit(solution)/shard_map/all_gather | solution.py:85
  9.9 103.9 %all-gather.3.cloned.1.call-start = ((), (), s32[]{:S(2)}) async-start(), calls=%async_computation.3 | async-start | bytes 2949120 | tf_op jit(solution)/shard_map/all_gather | solution.py:86
  12.3 139.3 %all-reduce.6.cloned.1.call-start = ((), (), s32[]{:S(2)}) async-start(), calls=%async_computation.8 | async-start | bytes 9437184 | tf_op jit(solution)/shard_map/psum | solution.py:98
  62.9 11.3 %copy-start.8 = (bf16[384,3072]{1,0:T(8,128)(2,1)S(1)}, bf16[384,3072]{1,0:T(8,128)(2,1)}, u32[]{:S(2)}) copy-start(bf16[384,3072]{1,0:T(8,128)(2,1)} %all-gather.5.cloned.1.call-done) | copy-start | bytes 7077892
  123.4 0.7 copy-start.6
  123.4 0.9 copy-start.5
  123.5 118.3 %reduce-scatter.6.cloned.1.call-start = ((), (), s32[]{:S(2)}) async-start(), calls=%async_computation.5 | async-start | bytes 2949120 | tf_op jit(solution)/shard_map/reduce_scatter | solution.py:112
  127.2 2.6 copy-start.7
  151.5 15.8 %copy-start.1 = (bf16[384,2048]{1,0:T(8,128)(2,1)S(1)}, bf16[384,2048]{1,0:T(8,128)(2,1)}, u32[]{:S(2)}) copy-start(bf16[384,2048]{1,0:T(8,128)(2,1)} %get-tuple-element.8) | copy-start | bytes 4718596
  167.4 12.2 %copy-start.2 = (bf16[384,2048]{1,0:T(8,128)(2,1)S(1)}, bf16[384,2048]{1,0:T(8,128)(2,1)}, u32[]{:S(2)}) copy-start(bf16[384,2048]{1,0:T(8,128)(2,1)} %get-tuple-element.9) | copy-start | bytes 4718596
  195.7 72.6 %reduce-scatter.10.cloned.1.call-start = ((), (), s32[]{:S(2)}) async-start(), calls=%async_computation.7 | async-start | bytes 40960
  198.0 149.2 %reduce-scatter.8.cloned.1.call-start = ((), (), s32[]{:S(2)}) async-start(), calls=%async_computation.6 | async-start | bytes 983040 | tf_op jit(solution)/shard_map/reduce_scatter | solution.py:122
  198.2 13.5 %copy-start.3 = (bf16[384,2048]{1,0:T(8,128)(2,1)S(1)}, bf16[384,2048]{1,0:T(8,128)(2,1)}, u32[]{:S(2)}) copy-start(bf16[384,2048]{1,0:T(8,128)(2,1)} %get-tuple-element.9) | copy-start | bytes 4718596
  198.3 13.5 %copy-start.4 = (bf16[384,2048]{1,0:T(8,128)(2,1)S(1)}, bf16[384,2048]{1,0:T(8,128)(2,1)}, u32[]{:S(2)}) copy-start(bf16[384,2048]{1,0:T(8,128)(2,1)} %get-tuple-element.7) | copy-start | bytes 4718596
  198.3 13.5 %copy-start.9 = (bf16[384,3072]{1,0:T(8,128)(2,1)S(1)}, bf16[384,3072]{1,0:T(8,128)(2,1)}, u32[]{:S(2)}) copy-start(bf16[384,3072]{1,0:T(8,128)(2,1)} %all-gather.5.cloned.1.call-done) | copy-start | bytes 7077892
Sparse Core Ops, SparseCore 0:
  10.1 52.6 all-gather.4
  65.0 48.7 all-gather.2
  123.6 27.9 all-reduce.5
  195.9 45.8 reduce-scatter.5
  244.9 23.4 reduce-scatter.9
  271.1 26.3 reduce-scatter.7
where the time goes:
time: 356 us
  waiting for transfers between devices  131 us (37%)
  matrix products  105 us (29%)
  blocking collectives  91.1 us (26%)
  between operations  15.6 us (4%)
  local copies, waits for them, and re-layouts  7.8 us (2%)
  other arithmetic  4.83 us (1%)
    psum x1, blocking collectives, shards(): router_grad = lax.psum(router_part, ('dp', 'expert'))  76.5 us
    all_gather x1, waiting for transfers between devices, shards(): lax.all_gather(local_tokens, 'dp', axis=0, tiled=True)  50.6 us
    dot_general x3, matrix products, contract_cols(): lax.dot_general(left_side, right_side, (((1,), (1,)), ((), ())), preferre...  38 us
    dot_general x3, matrix products, contract_rows(): lax.dot_general(left_side, right_side, (((0,), (0,)), ((), ())), preferre...  36 us
    all_gather x1, waiting for transfers between devices, shards(): lax.all_gather(local_grads, 'dp', axis=0, tiled=True)  30.3 us
    psum x1, waiting for transfers between devices, shards(): lax.psum(grad_part.astype(jnp.bfloat16), 'tensor').astype(jnp.float32)  20 us
    reduce_scatter x1, waiting for transfers between devices, shards(): lax.psum_scatter(slot_dx.astype(jnp.bfloat16), 'dp', scatter_dimension=0,...  19.6 us
    unnamed x1, blocking collectives  12.1 us
  transfers between devices with their start and end apart: 6, of which 5 were waited for; matrix products, arithmetic and copies ran while one was open for 20% of the time, Pallas kernels for 0%

commit v1 on v0

--- a/solution.py
+++ b/solution.py
@@ -146,7 +146,9 @@
         jnp.bfloat16
     )
     router_part = jnp.dot(part_tokens.astype(jnp.float32).T, logit_grad, precision=highest)
-    router_grad = lax.psum(router_part, ("dp", "expert"))
+    router_grad = router_part
+    for mesh_axis in ("expert", "dp"):
+        router_grad = lax.psum(router_grad, mesh_axis)
     return (tokens_grad, router_grad, gate_grad[None], up_grad[None], down_grad[None])
 
 

time: 356 us -> 316 us (0.89)
  blocking collectives: 91.1 us -> 50.6 us
    psum x1 -> x2, blocking collectives: 76.5 us -> 36 us  [shards(): router_grad = lax.psum(router_grad, mesh_axis)]
  transfers between devices with their start and end apart: 6 -> 6, of which waited for: 5 -> 5; matrix products, arithmetic and copies ran while one was open for 20% -> 22% of each run, Pallas kernels for 0% -> 0%
where the time goes in v1:
time: 316 us; the launch traced here: 315 us
  waiting for transfers between devices  131 us (41%)
  matrix products  105 us (33%)
  blocking collectives  50.6 us (16%)
  between operations  15.6 us (5%)
  local copies, waits for them, and re-layouts  7.8 us (2%)
  other arithmetic  4.83 us (2%)
    all_gather x1, waiting for transfers between devices, shards(): lax.all_gather(local_tokens, 'dp', axis=0, tiled=True)  50.6 us
    dot_general x3, matrix products, contract_cols(): lax.dot_general(left_side, right_side, (((1,), (1,)), ((), ())), preferre...  38 us
    dot_general x3, matrix products, contract_rows(): lax.dot_general(left_side, right_side, (((0,), (0,)), ((), ())), preferre...  36 us
    psum x2, blocking collectives, shards(): router_grad = lax.psum(router_grad, mesh_axis)  36 us
    all_gather x1, waiting for transfers between devices, shards(): lax.all_gather(local_grads, 'dp', axis=0, tiled=True)  30.2 us
    psum x1, waiting for transfers between devices, shards(): lax.psum(grad_part.astype(jnp.bfloat16), 'tensor').astype(jnp.float32)  20 us
    reduce_scatter x1, waiting for transfers between devices, shards(): lax.psum_scatter(slot_dx.astype(jnp.bfloat16), 'dp', scatter_dimension=0,...  19.6 us
    unnamed x1, blocking collectives  12.1 us
  transfers between devices with their start and end apart: 6, of which 5 were waited for; matrix products, arithmetic and copies ran while one was open for 22% of the time, Pallas kernels for 0%

profile of v1, /device:TPU:0, one launch (start us, length us, event | category | flops | bytes accessed | tf_op | source)
XLA Modules:
  0.0 315.4 jit_solution(14354826022559546774)
XLA Ops:
  7.2 0.0 copy-start
  7.2 0.0 all-gather.5.cloned.1.call-start
  7.2 0.8 slice_bitcast_fusion.1
  8.0 0.8 compare_bitcast_fusion.1
  8.8 1.1 convolution_convert_fusion
  9.9 0.0 all-gather.5.cloned.1.call-update
  9.9 0.0 all-gather.3.cloned.1.call-start
  10.0 2.3 convolution_convert_fusion.1
  12.2 0.0 all-gather.3.cloned.1.call-update
  12.3 0.0 all-reduce.6.cloned.1.call-start
  12.3 50.6 %all-gather.5.cloned.1.call-done = bf16[384,3072]{1,0:T(8,128)(2,1)} async-done(((bf16[96,3072]{1,0:T(8,128)(2,1)}), bf16[384,3072]{1,0:T(8,128)(2,1)}) %all-gather.5.cloned.1.call-update) | async-done | bytes 2359312 | tf_op jit(solution)/shard_map/all_gather | solution.py:85
  62.9 11.3 %fusion.31 = bf16[384,2048]{1,0:T(8,128)(2,1)} fusion(bf16[384,3072]{1,0:T(8,128)(2,1)} %all-gather.5.cloned.1.call-done, bf16[1,3072,2048]{2,1,0:T(8,128)(2,1)} %param.11), kind=kOutput, calls=%fused_computation.44 | convolution fusion | flops 4832624640 | bytes 16515072 | tf_op jit(solution)/shard_map/dot_general | solution.py:92
  74.1 9.4 %fusion.28 = bf16[384,2048]{1,0:T(8,128)(2,1)} fusion(bf16[384,3072]{1,0:T(8,128)(2,1)S(1)} %copy-done.8, bf16[1,3072,2048]{2,1,0:T(8,128)(2,1)} %param.12), kind=kOutput, calls=%fused_computation.43 | convolution fusion | flops 4832624640 | bytes 16515072 | tf_op jit(solution)/shard_map/dot_general | solution.py:93
  83.5 30.2 %all-gather.3.cloned.1.call-done = bf16[384,3072]{1,0:T(8,128)(2,1)} async-done(((bf16[96,3072]{1,0:T(8,128)(2,1)}), bf16[384,3072]{1,0:T(8,128)(2,1)}) %all-gather.3.cloned.1.call-update) | async-done | bytes 2359312 | tf_op jit(solution)/shard_map/all_gather | solution.py:86
  113.8 9.6 %fusion.25 = bf16[384,2048]{1,0:T(8,128)(2,1)} fusion(bf16[384,3072]{1,0:T(8,128)(2,1)} %all-gather.3.cloned.1.call-done, bf16[1,2048,3072]{2,1,0:T(8,128)(2,1)} %param.13), kind=kOutput, calls=%fused_computation.42 | convolution fusion | flops 4832624640 | bytes 16515072 | tf_op jit(solution)/shard_map/dot_general | solution.py:17
  123.4 0.0 all-reduce.6.cloned.1.call-update
  123.5 0.0 reduce-scatter.6.cloned.1.call-start
  123.5 0.6 copy-done.6
  124.1 0.1 copy.59
  124.2 0.1 reshape.58
  124.4 0.3 fusion.66
  124.7 2.5 psum.42
  127.2 2.4 gather_fusion
  129.5 0.1 reshape.61
  129.7 0.1 copy.60
  129.7 0.6 fusion.65
  131.1 0.1 convolution_bitcast_fusion.3
  131.2 0.1 fusion.37
  131.3 0.2 dynamic-update-slice
  131.5 20.0 %all-reduce.6.cloned.1.call-done = (bf16[384,2048]{1,0:T(8,128)(2,1)}, bf16[384,2048]{1,0:T(8,128)(2,1)}, bf16[384,2048]{1,0:T(8,128)(2,1)}) async-done(((bf16[384,2048]{1,0:T(8,128)(2,1)}, bf16[384,2048]{1,0:T(8,128)(2,1)}, bf16[384,2048]{1,0:T(8,128)(2,1)}), (bf16[384,2048]{1,0:T(8,128)(2,1)}, bf16[384,2048]{1,0:T(8,128)(2,1)}, bf16[384,2048]{1,0:T(8,128)(2,1)})) %all-reduce.6.cloned.1.call-update) | async-done | bytes 4718608 | tf_op jit(solution)/shard_map/psum | solution.py:98
  151.5 3.7 %fusion.14 = bf16[384]{0:T(512)(128)(2,1)S(1)} fusion(bf16[384,2048]{1,0:T(8,128)(2,1)} %get-tuple-element.7, bf16[384,2048]{1,0:T(8,128)(2,1)} %get-tuple-element.8, bf16[384,2048]{1,0:T(8,128)(2,1)} %get-tuple-element.9), kind=kLoop, calls=%fused_computation.31 | loop fusion | flops 9436800 | bytes 4719360 | tf_op jit(solution)/shard_map/reduce_sum | solution.py:49
  155.2 12.1 %all-reduce.2 = (bf16[384]{0:T(512)(128)(2,1)S(1)}, bf16[384]{0:T(512)(128)(2,1)S(1)}) all-reduce(bf16[384]{0:T(512)(128)(2,1)S(1)} %fusion.14, bf16[384]{0:T(512)(128)(2,1)S(1)} %dynamic-update-slice), channel_id=4, replica_groups=mesh['dp'=4,'expert'=4,'tensor'=2] {'dp'}, use_global_device_ids=true, to_apply=%region_7.8.clone | all-reduce | flops 768 | bytes 3072
  167.4 12.2 %fusion = f32[384,3072]{1,0:T(8,128)} fusion(bf16[1,3072,2048]{2,1,0:T(8,128)(2,1)} %param.11, bf16[384,2048]{1,0:T(8,128)(2,1)S(1)} %copy-done.1, bf16[384,2048]{1,0:T(8,128)(2,1)} %get-tuple-element.7, bf16[384,2048]{1,0:T(8,128)(2,1)} %get-tuple-element.9, f32[384]{0:T(512)S(1)} %convert_element_type.124), kind=kOutput, calls=%fused_computation.2 | convolution fusion | flops 4842848256 | bytes 22021632 | tf_op jit(solution)/shard_map/dot_general | solution.py:17
  179.6 16.1 %add_convert_fusion = bf16[384,3072]{1,0:T(8,128)(2,1)} fusion(f32[384,3072]{1,0:T(8,128)} %fusion, bf16[1,3072,2048]{2,1,0:T(8,128)(2,1)} %param.12, bf16[384,2048]{1,0:T(8,128)(2,1)S(1)} %copy-done.2, bf16[384,2048]{1,0:T(8,128)(2,1)} %get-tuple-element.7, f32[384]{0:T(512)S(1)} %convert_element_type.124), kind=kOutput, calls=%fused_computation.20 | convolution fusion | flops 4841275392 | bytes 22808064 | tf_op jit(solution)/shard_map/dot_general | solution.py:17
  195.7 0.0 reduce-scatter.6.cloned.1.call-update
  195.7 0.0 reduce-scatter.10.cloned.1.call-start
  195.8 0.1 bitcast_or_fusion
  195.9 0.1 copy.61
  195.9 0.1 reshape.64
  196.7 0.2 convolution_bitcast_fusion.1
  196.9 0.2 fusion.35
  197.1 0.1 multiply_convert_fusion.2
  197.2 0.7 copy.63
  197.9 0.0 reduce-scatter.10.cloned.1.call-update
  198.0 0.3 reduce-scatter.8.cloned.1.call-start
  198.3 13.5 %convert_bitcast_fusion.2 = bf16[1,3072,2048]{2,1,0:T(8,128)(2,1)} fusion(bf16[384,3072]{1,0:T(8,128)(2,1)} %all-gather.5.cloned.1.call-done, bf16[384,2048]{1,0:T(8,128)(2,1)S(1)} %copy-done.1, bf16[384,2048]{1,0:T(8,128)(2,1)} %get-tuple-element.7, bf16[384,2048]{1,0:T(8,128)(2,1)} %get-tuple-element.9, f32[384]{0:T(512)S(1)} %convert_element_type.124), kind=kOutput, calls=%fused_computation.14 | convolution fusion | flops 4849139712 | bytes 19662336 | tf_op jit(solution)/shard_map/dot_general | solution.py:11
  211.7 0.0 copy-done.3
  211.8 10.3 %convert_bitcast_fusion.1 = bf16[1,3072,2048]{2,1,0:T(8,128)(2,1)} fusion(bf16[384,3072]{1,0:T(8,128)(2,1)S(1)} %copy-done.9, bf16[384,2048]{1,0:T(8,128)(2,1)S(1)} %copy-done.3, bf16[384,2048]{1,0:T(8,128)(2,1)S(1)} %copy-done.4, f32[384]{0:T(512)S(1)} %convert_element_type.124), kind=kOutput, calls=%fused_computation.13 | convolution fusion | flops 4845207552 | bytes 18089472 | tf_op jit(solution)/shard_map/dot_general | solution.py:11
  222.1 19.6 %reduce-scatter.6.cloned.1.call-done = bf16[96,3072]{1,0:T(8,128)(2,1)} async-done(((bf16[384,3072]{1,0:T(8,128)(2,1)}), bf16[96,3072]{1,0:T(8,128)(2,1)}) %reduce-scatter.6.cloned.1.call-update) | async-done | bytes 589840 | tf_op jit(solution)/shard_map/reduce_scatter | solution.py:112
  241.7 1.5 fusion.48
  243.2 2.4 fusion.12
  245.6 0.0 reduce-scatter.8.cloned.1.call-update
  245.6 12.1 %convert_bitcast_fusion = bf16[1,2048,3072]{2,1,0:T(8,128)(2,1)} fusion(bf16[384,3072]{1,0:T(8,128)(2,1)} %all-gather.3.cloned.1.call-done, f32[384]{0:T(512)S(1)} %convert_element_type.124, bf16[384,2048]{1,0:T(8,128)(2,1)S(1)} %copy-done.1, bf16[384,2048]{1,0:T(8,128)(2,1)} %get-tuple-element.9), kind=kOutput, calls=%fused_computation.12 | convolution fusion | flops 4847960064 | bytes 18089472 | tf_op jit(solution)/shard_map/dot_general | solution.py:11
  257.7 10.6 %reduce-scatter.10.cloned.1.call-done = bf16[32,4]{1,0:T(8,128)(2,1)} async-done(((bf16[128,4]{1,0:T(8,128)(2,1)}), bf16[32,4]{1,0:T(8,128)(2,1)}) %reduce-scatter.10.cloned.1.call-update) | async-done | bytes 272
  268.3 0.8 copy.64
  269.1 0.9 gather_fusion.1
  270.0 0.1 reshape.67
  270.1 0.1 copy.62
  270.2 0.1 multiply_reduce_fusion
  270.3 0.1 subtract_multiply_fusion
  270.4 0.2 fusion.38
  270.6 15.9 %psum.46 = f32[3072,4]{0,1:T(4,128)S(1)} all-reduce(f32[3072,4]{0,1:T(4,128)S(1)} %fusion.38), channel_id=1, replica_groups=mesh['dp'=4,'expert'=4,'tensor'=2] {'expert'}, use_global_device_ids=true, to_apply=%region_11.12 | all-reduce | flops 12288 | bytes 98304 | tf_op jit(solution)/shard_map/psum | solution.py:151
  286.6 20.0 %psum.47 = f32[3072,4]{0,1:T(4,128)} all-reduce(f32[3072,4]{0,1:T(4,128)S(1)} %psum.46), channel_id=1, replica_groups=mesh['dp'=4,'expert'=4,'tensor'=2] {'dp'}, use_global_device_ids=true, to_apply=%region_12.13 | all-reduce | flops 12288 | bytes 98304 | tf_op jit(solution)/shard_map/psum | solution.py:151
  306.6 2.0 fusion.13
  (28 shorter events, 0.1 us)
Async XLA Ops:
  7.2 1.6 copy-start
  7.2 55.7 %all-gather.5.cloned.1.call-start = ((), (), s32[]{:S(2)}) async-start(), calls=%async_computation.4 | async-start | bytes 2949120 | tf_op jit(solution)/shard_map/all_gather | solution.py:85
  9.9 103.9 %all-gather.3.cloned.1.call-start = ((), (), s32[]{:S(2)}) async-start(), calls=%async_computation.3 | async-start | bytes 2949120 | tf_op jit(solution)/shard_map/all_gather | solution.py:86
  12.3 139.3 %all-reduce.6.cloned.1.call-start = ((), (), s32[]{:S(2)}) async-start(), calls=%async_computation.8 | async-start | bytes 9437184 | tf_op jit(solution)/shard_map/psum | solution.py:98
  62.9 11.3 %copy-start.8 = (bf16[384,3072]{1,0:T(8,128)(2,1)S(1)}, bf16[384,3072]{1,0:T(8,128)(2,1)}, u32[]{:S(2)}) copy-start(bf16[384,3072]{1,0:T(8,128)(2,1)} %all-gather.5.cloned.1.call-done) | copy-start | bytes 7077892
  123.4 0.7 copy-start.6
  123.4 0.9 copy-start.5
  123.5 118.3 %reduce-scatter.6.cloned.1.call-start = ((), (), s32[]{:S(2)}) async-start(), calls=%async_computation.5 | async-start | bytes 2949120 | tf_op jit(solution)/shard_map/reduce_scatter | solution.py:112
  127.2 2.6 copy-start.7
  151.5 15.8 %copy-start.1 = (bf16[384,2048]{1,0:T(8,128)(2,1)S(1)}, bf16[384,2048]{1,0:T(8,128)(2,1)}, u32[]{:S(2)}) copy-start(bf16[384,2048]{1,0:T(8,128)(2,1)} %get-tuple-element.8) | copy-start | bytes 4718596
  167.4 12.2 %copy-start.2 = (bf16[384,2048]{1,0:T(8,128)(2,1)S(1)}, bf16[384,2048]{1,0:T(8,128)(2,1)}, u32[]{:S(2)}) copy-start(bf16[384,2048]{1,0:T(8,128)(2,1)} %get-tuple-element.9) | copy-start | bytes 4718596
  195.7 72.6 %reduce-scatter.10.cloned.1.call-start = ((), (), s32[]{:S(2)}) async-start(), calls=%async_computation.7 | async-start | bytes 40960
  198.0 108.6 %reduce-scatter.8.cloned.1.call-start = ((), (), s32[]{:S(2)}) async-start(), calls=%async_computation.6 | async-start | bytes 983040 | tf_op jit(solution)/shard_map/reduce_scatter | solution.py:122
  198.2 13.5 %copy-start.3 = (bf16[384,2048]{1,0:T(8,128)(2,1)S(1)}, bf16[384,2048]{1,0:T(8,128)(2,1)}, u32[]{:S(2)}) copy-start(bf16[384,2048]{1,0:T(8,128)(2,1)} %get-tuple-element.9) | copy-start | bytes 4718596
  198.2 13.5 %copy-start.4 = (bf16[384,2048]{1,0:T(8,128)(2,1)S(1)}, bf16[384,2048]{1,0:T(8,128)(2,1)}, u32[]{:S(2)}) copy-start(bf16[384,2048]{1,0:T(8,128)(2,1)} %get-tuple-element.7) | copy-start | bytes 4718596
  198.2 13.5 %copy-start.9 = (bf16[384,3072]{1,0:T(8,128)(2,1)S(1)}, bf16[384,3072]{1,0:T(8,128)(2,1)}, u32[]{:S(2)}) copy-start(bf16[384,3072]{1,0:T(8,128)(2,1)} %all-gather.5.cloned.1.call-done) | copy-start | bytes 7077892
Sparse Core Ops, SparseCore 0:
  10.1 52.6 all-gather.4
  65.0 48.7 all-gather.2
  123.6 27.9 all-reduce.5
  195.8 45.8 reduce-scatter.5
  244.9 23.4 reduce-scatter.9
  271.1 26.2 reduce-scatter.7
